TPU v7x, 8 devices: a whole 2x2x1 slice. The times are simulated.
8 devices in a mesh: dp: 1 (over z), tp: 8 (over x, y, core).
Axes of the slice: x: 2, y: 2, z: 1, core: 2. Of those that a mesh axis runs over, the one named last changes fastest.
Arguments:
- x: bfloat16 [4096, 2048], P(('dp', 'tp'))
- w_gate: bfloat16 [2048, 8192], P(None, 'tp')
- w_up: bfloat16 [2048, 8192], P(None, 'tp')
- w_down: bfloat16 [8192, 2048], P('tp')
Outputs:
- output: bfloat16 [4096, 2048], P(('dp', 'tp'))
All inputs are finite; a program needn't handle non-finite values.
Results may differ from a plain program's by a relative error of at most 0.016.
Values are sent between devices in bfloat16 or wider.
A program may use at most 2 GiB of HBM per device.

v0:
```python
import jax
import jax.numpy as jnp
from jax import lax
from jax.sharding import PartitionSpec as P


def solution(mesh):
    def step(x, w_gate, w_up, w_down):
        rows = lax.all_gather(x, "tp", axis=0, tiled=True)
        gate = jnp.dot(rows, w_gate, preferred_element_type=jnp.float32)
        up = jnp.dot(rows, w_up, preferred_element_type=jnp.float32)
        hidden = (jax.nn.silu(gate) * up).astype(jnp.bfloat16)
        term = jnp.dot(hidden, w_down, preferred_element_type=jnp.float32).astype(jnp.bfloat16)
        return lax.psum_scatter(term, "tp", scatter_dimension=0, tiled=True)

    return jax.shard_map(
        step,
        mesh=mesh,
        in_specs=(P(("dp", "tp"), None), P(None, "tp"), P(None, "tp"), P("tp", None)),
        out_specs=P(("dp", "tp"), None),
        check_vma=False,
    )
```

profile of v0, /device:TPU:7, one launch (start us, length us, event | category | flops | bytes accessed | tf_op | source)
XLA Modules:
  0.0 283.5 jit_solution(15101760765370608343)
XLA Ops:
  6.5 0.0 all-gather.2.cloned.1.call-start
  6.5 0.7 all-gather.2.cloned.1.call-update
  7.3 0.0 reduce-scatter.2.cloned.1.call-start
  7.3 86.4 %all-gather.2.cloned.1.call-done = bf16[4096,2048]{1,0:T(8,128)(2,1)} async-done(((bf16[512,2048]{1,0:T(8,128)(2,1)}), bf16[4096,2048]{1,0:T(8,128)(2,1)}) %all-gather.2.cloned.1.call-update) | async-done | bytes 16777232 | tf_op jit(solution)/shard_map/all_gather | solution.py:9
  93.7 0.0 copy-start
  93.7 23.5 %fusion.1 = f32[4096,1024]{1,0:T(8,128)} fusion(bf16[4096,2048]{1,0:T(8,128)(2,1)} %all-gather.2.cloned.1.call-done, bf16[2048,1024]{1,0:T(8,128)(2,1)} %param.5), kind=kOutput, calls=%fused_computation.3 | convolution fusion | flops 17179869184 | bytes 37748736 | tf_op jit(solution)/shard_map/dot_general | solution.py:10
  117.2 0.0 copy-done
  117.2 0.0 copy-start.1
  117.2 29.4 %multiply_convert_fusion.clone.4 = bf16[4096,1024]{1,0:T(8,128)(2,1)} fusion(f32[4096,1024]{1,0:T(8,128)} %fusion.1, bf16[4096,2048]{1,0:T(8,128)(2,1)} %all-gather.2.cloned.1.call-done, bf16[2048,1024]{1,0:T(8,128)(2,1)S(1)} %copy-done), kind=kOutput, calls=%fused_computation.clone.clone.clone.1 | convolution fusion | flops 17205035008 | bytes 46137344 | tf_op jit(solution)/shard_map/dot_general | solution.py:11
  146.6 0.0 copy-done.1
  146.6 23.7 %convolution_convert_fusion = bf16[4096,2048]{1,0:T(8,128)(2,1)} fusion(bf16[1024,2048]{1,0:T(8,128)(2,1)S(1)} %copy-done.1, bf16[4096,1024]{1,0:T(8,128)(2,1)} %multiply_convert_fusion.clone.4), kind=kOutput, calls=%fused_computation.1 | convolution fusion | flops 17188257792 | bytes 29360128 | tf_op jit(solution)/shard_map/dot_general | solution.py:13
  170.2 0.0 reduce-scatter.2.cloned.1.call-update
  170.3 106.4 %reduce-scatter.2.cloned.1.call-done = bf16[512,2048]{1,0:T(8,128)(2,1)} async-done(((bf16[4096,2048]{1,0:T(8,128)(2,1)}), bf16[512,2048]{1,0:T(8,128)(2,1)}) %reduce-scatter.2.cloned.1.call-update) | async-done | bytes 2097168 | tf_op jit(solution)/shard_map/reduce_scatter | solution.py:14
Async XLA Ops:
  6.5 87.1 %all-gather.2.cloned.1.call-start = ((), (), s32[]{:S(2)}) async-start(), calls=%async_computation.1 | async-start | bytes 18874368 | tf_op jit(solution)/shard_map/all_gather | solution.py:9
  7.3 269.4 %reduce-scatter.2.cloned.1.call-start = ((), (), s32[]{:S(2)}) async-start(), calls=%async_computation.2 | async-start | bytes 18874368 | tf_op jit(solution)/shard_map/reduce_scatter | solution.py:14
  93.7 23.5 %copy-start = (bf16[2048,1024]{1,0:T(8,128)(2,1)S(1)}, bf16[2048,1024]{1,0:T(8,128)(2,1)}, u32[]{:S(2)}) copy-start(bf16[2048,1024]{1,0:T(8,128)(2,1)} %param.6) | copy-start | bytes 12582916
  117.2 29.4 %copy-start.1 = (bf16[1024,2048]{1,0:T(8,128)(2,1)S(1)}, bf16[1024,2048]{1,0:T(8,128)(2,1)}, u32[]{:S(2)}) copy-start(bf16[1024,2048]{1,0:T(8,128)(2,1)} %param.7) | copy-start | bytes 12582916
Sparse Core Ops, SparseCore 0:
  9.1 84.4 all-gather.1
  170.4 106.2 reduce-scatter.1
where the time goes:
time: 287 us; the launch traced here: 284 us
  waiting for transfers between devices  193 us (67%)
  matrix products  76.6 us (27%)
  between operations  13.4 us (5%)
    reduce_scatter x1, waiting for transfers between devices, step(): return lax.psum_scatter(term, 'tp', scatter_dimension=0, tiled=True)  106 us
    all_gather x1, waiting for transfers between devices, step(): rows = lax.all_gather(x, 'tp', axis=0, tiled=True)  86.4 us
    dot_general x1, matrix products, step(): up = jnp.dot(rows, w_up, preferred_element_type=jnp.float32)  29.4 us
    dot_general x1, matrix products, step(): jnp.dot(hidden, w_down, preferred_element_type=jnp.float32)  23.7 us
    dot_general x1, matrix products, step(): gate = jnp.dot(rows, w_gate, preferred_element_type=jnp.float32)  23.5 us
  transfers between devices with their start and end apart: 2, of which 2 were waited for; matrix products, arithmetic and copies ran while one was open for 0% of the time, Pallas kernels for 0%

commit v1 on v0

v1 whole, which is shorter than its diff:
```python
import jax
import jax.numpy as jnp
from jax import lax
from jax.experimental import pallas as pl
from jax.experimental.pallas import tpu as pltpu
from jax.sharding import PartitionSpec as P

BF16 = jnp.bfloat16
F32 = jnp.float32

SUB = 128
UNIT = 256
TILE = 256

OWN, BX, BY, BD = 0, 1, 2, 3


def kernel(
    x_hbm, wg_hbm, wu_hbm, wd_hbm, out_hbm,
    wg, wu, wd, xb, hid, pd, px, py, px32, py32, sx, sy, own, relx, rely, finx, finy, out,
    loc_sem, out_sem, w_send, w_recv, ag_send, ag_recv, fw_send, fw_recv, d_send, d_recv, f_send, f_recv,
):
    half = wg_hbm.shape[1]
    width = wd_hbm.shape[1]
    tiles = half // TILE

    me = lax.axis_index("tp")
    core = me % 2
    iy = (me // 2) % 2
    nx = (me + 4) % 8
    ny = me + 2 - 4 * iy
    sib = me + 1 - 2 * core

    local = [
        pltpu.make_async_copy(wg_hbm, wg.at[0], loc_sem.at[0]),
        pltpu.make_async_copy(wu_hbm, wu.at[0], loc_sem.at[1]),
        pltpu.make_async_copy(wd_hbm, wd.at[pl.ds(0, half)], loc_sem.at[2]),
        pltpu.make_async_copy(x_hbm, xb.at[OWN], loc_sem.at[3]),
    ]
    for c in local:
        c.start()

    barrier = pltpu.get_barrier_semaphore()
    for d in (nx, ny, sib):
        pl.semaphore_signal(barrier, inc=1, device_id={"tp": d}, device_id_type=pl.DeviceIdType.MESH)
    pl.semaphore_wait(barrier, 3)

    def remote(src, dst, send, recv, d):
        return pltpu.make_async_remote_copy(
            src_ref=src, dst_ref=dst, send_sem=send, recv_sem=recv,
            device_id={"tp": d}, device_id_type=pl.DeviceIdType.MESH,
        )

    def rows(i):
        return pl.ds(i * SUB, SUB)

    order_x, order_y = (0, 1, 2, 3), (2, 3, 0, 1)
    ag_x = {i: remote(x_hbm.at[rows(i)], xb.at[BX, rows(i)], ag_send.at[0, i], ag_recv.at[0, i], nx) for i in order_x}
    ag_y = {i: remote(x_hbm.at[rows(i)], xb.at[BY, rows(i)], ag_send.at[1, i], ag_recv.at[1, i], ny) for i in order_y}
    for i, j in zip(order_x, order_y):
        ag_x[i].start()
        ag_y[j].start()
    swap = [
        remote(wg_hbm, wg.at[1], w_send.at[0], w_recv.at[0], sib),
        remote(wu_hbm, wu.at[1], w_send.at[1], w_recv.at[1], sib),
        remote(wd_hbm, wd.at[pl.ds(half, half)], w_send.at[2], w_recv.at[2], sib),
    ]
    for c in swap:
        c.start()

    fw_y = [remote(xb.at[BX, rows(k)], xb.at[BD, rows(2 * k)], fw_send.at[1, k], fw_recv.at[1, k], ny) for k in range(2)]
    fw_x = [remote(xb.at[BY, rows(2 + k)], xb.at[BD, rows(2 * k + 1)], fw_send.at[0, k], fw_recv.at[0, k], nx) for k in range(2)]
    for k in range(2):
        ag_x[k].wait_recv()
        fw_y[k].start()
        ag_y[2 + k].wait_recv()
        fw_x[k].start()

    def block(x_ref, write):
        def hidden(n, _):
            s, col = n // tiles, pl.multiple_of((n % tiles) * TILE, TILE)
            gate = jnp.dot(x_ref[...], wg[s, :, pl.ds(col, TILE)], preferred_element_type=F32)
            up = jnp.dot(x_ref[...], wu[s, :, pl.ds(col, TILE)], preferred_element_type=F32)
            hid[:, pl.ds(pl.multiple_of(n * TILE, TILE), TILE)] = (jax.nn.silu(gate) * up).astype(BF16)
            return _

        def down(n, _):
            cols = pl.ds(pl.multiple_of(n * TILE, TILE), TILE)
            write(cols, jnp.dot(hid[...], wd[:, cols], preferred_element_type=F32))
            return _

        lax.fori_loop(0, 2 * tiles, hidden, None)
        lax.fori_loop(0, width // TILE, down, None)

    def into(ref, r0):
        def write(cols, v):
            ref[pl.ds(r0, UNIT), cols] = v.astype(ref.dtype)

        return write

    def unit(b, u, ref, r0):
        block(xb.at[b, pl.ds(u * UNIT, UNIT)], into(ref, r0))

    for c in local[:3]:
        c.wait()
    for c in swap:
        c.wait_recv()

    fin_x = {i: remote((px if i < 2 else sx).at[rows(i % 2)], finx.at[rows(i)], f_send.at[0, i], f_recv.at[0, i], nx) for i in range(4)}
    fin_y = {i: remote((sy if i < 2 else py).at[rows(i % 2)], finy.at[rows(i)], f_send.at[1, i], f_recv.at[1, i], ny) for i in range(4)}
    d_x = [remote(pd.at[rows(2 * k)], relx.at[rows(k)], d_send.at[0, k], d_recv.at[0, k], nx) for k in range(2)]
    d_y = [remote(pd.at[rows(2 * k + 1)], rely.at[rows(k)], d_send.at[1, k], d_recv.at[1, k], ny) for k in range(2)]

    unit(BX, 0, px, 0)
    for i in (0, 1):
        fin_x[i].start()
    unit(BY, 1, py, 0)
    for i in (2, 3):
        fin_y[i].start()
    local[3].wait()
    unit(OWN, 0, own, 0)
    for i in (2, 3):
        ag_x[i].wait_recv()
    unit(BX, 1, px32, 0)
    fw_y[0].wait_recv()
    fw_x[0].wait_recv()
    unit(BD, 0, pd, 0)
    d_x[0].start()
    d_y[0].start()
    for i in (0, 1):
        ag_y[i].wait_recv()
    unit(BY, 0, py32, 0)
    fw_y[1].wait_recv()
    fw_x[1].wait_recv()
    unit(BD, 1, pd, UNIT)
    d_x[1].start()
    d_y[1].start()
    unit(OWN, 1, own, UNIT)

    for i in (0, 1):
        fin_x[i].wait_recv()
        own[rows(i)] += finx[rows(i)].astype(F32)
    for i in (2, 3):
        fin_y[i].wait_recv()
        own[rows(i)] += finy[rows(i)].astype(F32)

    for k in range(2):
        d_x[k].wait_recv()
        sy[rows(k)] = (py32[rows(k)] + relx[rows(k)].astype(F32)).astype(BF16)
        fin_y[k].start()
        d_y[k].wait_recv()
        sx[rows(k)] = (px32[rows(k)] + rely[rows(k)].astype(F32)).astype(BF16)
        fin_x[2 + k].start()

    writes = []
    for k in range(2):
        for fin, ref, i in ((fin_x, finx, 2 + k), (fin_y, finy, k)):
            fin[i].wait_recv()
            out[rows(i)] = (own[rows(i)] + ref[rows(i)].astype(F32)).astype(BF16)
            c = pltpu.make_async_copy(out.at[rows(i)], out_hbm.at[rows(i)], out_sem.at[i])
            c.start()
            writes.append(c)

    for c in (*ag_x.values(), *ag_y.values(), *swap, *fw_x, *fw_y, *d_x, *d_y, *fin_x.values(), *fin_y.values()):
        c.wait_send()
    for c in writes:
        c.wait()


def solution(mesh):
    def step(x, w_gate, w_up, w_down):
        rows, depth = x.shape
        half, width = w_down.shape
        vmem = pltpu.VMEM
        dma = pltpu.SemaphoreType.DMA
        flops = 2 * 4 * rows * depth * 2 * half * 3
        return pl.pallas_call(
            kernel,
            out_shape=jax.ShapeDtypeStruct((rows, width), BF16),
            in_specs=[pl.BlockSpec(memory_space=pl.ANY)] * 4,
            out_specs=pl.BlockSpec(memory_space=pl.ANY),
            scratch_shapes=[
                vmem((2, depth, half), BF16),
                vmem((2, depth, half), BF16),
                vmem((2 * half, width), BF16),
                vmem((4, rows, depth), BF16),
                vmem((UNIT, 2 * half), BF16),
                vmem((rows, width), BF16),
                vmem((UNIT, width), BF16),
                vmem((UNIT, width), BF16),
                vmem((UNIT, width), F32),
                vmem((UNIT, width), F32),
                vmem((UNIT, width), BF16),
                vmem((UNIT, width), BF16),
                vmem((rows, width), F32),
                vmem((UNIT, width), BF16),
                vmem((UNIT, width), BF16),
                vmem((rows, width), BF16),
                vmem((rows, width), BF16),
                vmem((rows, width), BF16),
                dma((4,)),
                dma((4,)),
                dma((3,)),
                dma((3,)),
                dma((2, 4)),
                dma((2, 4)),
                dma((2, 2)),
                dma((2, 2)),
                dma((2, 2)),
                dma((2, 2)),
                dma((2, 4)),
                dma((2, 4)),
            ],
            compiler_params=pltpu.CompilerParams(
                collective_id=0, has_side_effects=True, vmem_limit_bytes=67_000_000
            ),
            cost_estimate=pl.CostEstimate(flops=flops, bytes_accessed=32 * 2**20, transcendentals=0),
            name="mlp",
        )(x, w_gate, w_up, w_down)

    return jax.shard_map(
        step,
        mesh=mesh,
        in_specs=(P(("dp", "tp"), None), P(None, "tp"), P(None, "tp"), P("tp", None)),
        out_specs=P(("dp", "tp"), None),
        check_vma=False,
    )
```

time: 287 us -> 145 us (0.51)
  the two profiles are of different devices: /device:TPU:7 before, /device:TPU:0 now
where the time goes in v1:
time: 145 us
  Pallas kernels  142 us (98%)
  local copies, waits for them, and re-layouts  3.16 us (2%)
    pallas_call x1, Pallas kernels, step(): pl.pallas_call(kernel, out_shape=jax.ShapeDtypeStruct((rows, width), BF16...  142 us
    unnamed x1, local copies, waits for them, and re-layouts  3.16 us

profile of v1, /device:TPU:0, one launch (start us, length us, event | category | flops | bytes accessed | tf_op | source)
XLA Modules:
  0.0 144.9 jit_solution(11630344987349717610)
XLA Ops:
  0.0 141.7 %mlp.1 = bf16[512,2048]{1,0:T(8,128)(2,1)} custom-call(bf16[512,2048]{1,0:T(8,128)(2,1)} %x_hbm.1, bf16[2048,1024]{1,0:T(8,128)(2,1)} %wg_hbm.1, bf16[2048,1024]{1,0:T(8,128)(2,1)} %wu_hbm.1, bf16[1024,2048]{1,0:T(8,128)(2,1)} %wd_hbm.1), custom_call_target="tpu_custom_call" | custom-call | flops 51539607552 | bytes 33554432 | tf_op jit(solution)/shard_map/mlp/pallas_call | solution.py:177
  141.7 3.2 %copy.6 = bf16[512,2048]{1,0:T(8,128)(2,1)} copy(bf16[512,2048]{1,0:T(8,128)(2,1)} %mlp.1) | data formatting | bytes 4194304

commit v2 on v1

--- a/solution.py
+++ b/solution.py
@@ -16,9 +16,9 @@
 
 
 def kernel(
-    x_hbm, wg_hbm, wu_hbm, wd_hbm, out_hbm,
-    wg, wu, wd, xb, hid, pd, px, py, px32, py32, sx, sy, own, relx, rely, finx, finy, out,
-    loc_sem, out_sem, w_send, w_recv, ag_send, ag_recv, fw_send, fw_recv, d_send, d_recv, f_send, f_recv,
+    x_hbm, wg_hbm, wu_hbm, wd_hbm, out,
+    wg, wu, wd, xb, hid, pd, px, py, px32, py32, sx, sy, own, relx, rely, finx, finy,
+    loc_sem, w_send, w_recv, ag_send, ag_recv, fw_send, fw_recv, d_send, d_recv, f_send, f_recv,
 ):
     half = wg_hbm.shape[1]
     width = wd_hbm.shape[1]
@@ -152,19 +152,13 @@
         sx[rows(k)] = (px32[rows(k)] + rely[rows(k)].astype(F32)).astype(BF16)
         fin_x[2 + k].start()
 
-    writes = []
     for k in range(2):
         for fin, ref, i in ((fin_x, finx, 2 + k), (fin_y, finy, k)):
             fin[i].wait_recv()
             out[rows(i)] = (own[rows(i)] + ref[rows(i)].astype(F32)).astype(BF16)
-            c = pltpu.make_async_copy(out.at[rows(i)], out_hbm.at[rows(i)], out_sem.at[i])
-            c.start()
-            writes.append(c)
 
     for c in (*ag_x.values(), *ag_y.values(), *swap, *fw_x, *fw_y, *d_x, *d_y, *fin_x.values(), *fin_y.values()):
         c.wait_send()
-    for c in writes:
-        c.wait()
 
 
 def solution(mesh):
@@ -176,9 +170,9 @@
         flops = 2 * 4 * rows * depth * 2 * half * 3
         return pl.pallas_call(
             kernel,
-            out_shape=jax.ShapeDtypeStruct((rows, width), BF16),
+            out_shape=pltpu.VMEM((rows, width), BF16),
             in_specs=[pl.BlockSpec(memory_space=pl.ANY)] * 4,
-            out_specs=pl.BlockSpec(memory_space=pl.ANY),
+            out_specs=pl.BlockSpec(memory_space=pltpu.VMEM),
             scratch_shapes=[
                 vmem((2, depth, half), BF16),
                 vmem((2, depth, half), BF16),
@@ -197,8 +191,6 @@
                 vmem((UNIT, width), BF16),
                 vmem((rows, width), BF16),
                 vmem((rows, width), BF16),
-                vmem((rows, width), BF16),
-                dma((4,)),
                 dma((4,)),
                 dma((3,)),
                 dma((3,)),
@@ -212,7 +204,7 @@
                 dma((2, 4)),
             ],
             compiler_params=pltpu.CompilerParams(
-                collective_id=0, has_side_effects=True, vmem_limit_bytes=67_000_000
+                collective_id=0, has_side_effects=True, vmem_limit_bytes=60 * 2**20
             ),
             cost_estimate=pl.CostEstimate(flops=flops, bytes_accessed=32 * 2**20, transcendentals=0),
             name="mlp",

time: 145 us -> 142 us (0.979)
  local copies, waits for them, and re-layouts: 3.16 us -> 1.32 us
    unnamed x1, local copies, waits for them, and re-layouts: 3.16 us -> 1.32 us
where the time goes in v2:
time: 142 us
  Pallas kernels  141 us (99%)
    pallas_call x1, Pallas kernels, step(): pl.pallas_call(kernel, out_shape=pltpu.VMEM((rows, width), BF16), in_spec...  141 us

profile of v2, /device:TPU:0, one launch (start us, length us, event | category | flops | bytes accessed | tf_op | source)
XLA Modules:
  0.0 142.2 jit_solution(4668451328739453405)
XLA Ops:
  0.0 140.8 %mlp.1 = bf16[512,2048]{1,0:T(8,128)(2,1)S(1)} custom-call(bf16[512,2048]{1,0:T(8,128)(2,1)} %x_hbm.1, bf16[2048,1024]{1,0:T(8,128)(2,1)} %wg_hbm.1, bf16[2048,1024]{1,0:T(8,128)(2,1)} %wu_hbm.1, bf16[1024,2048]{1,0:T(8,128)(2,1)} %wd_hbm.1), custom_call_target="tpu_custom_call" | custom-call | flops 51539607552 | bytes 33554432 | tf_op jit(solution)/shard_map/mlp/pallas_call | solution.py:171
  140.8 1.3 copy.6

commit v3 on v2

v3 whole, which is shorter than its diff:
```python
import jax
import jax.numpy as jnp
from jax import lax
from jax.experimental import pallas as pl
from jax.experimental.pallas import tpu as pltpu
from jax.sharding import PartitionSpec as P

BF16 = jnp.bfloat16
F32 = jnp.float32
MESH = pl.DeviceIdType.MESH

SUB = 128
UNIT = 256
TILE = 256

OWN, BX, BY, BD = 0, 1, 2, 3

RELAY = ((0, 128, 0), (128, 96, 1), (224, 32, 1))


def kernel(
    x_hbm, wg_hbm, wu_hbm, wd_hbm, out,
    w, wd, xb, hid, pd, px, py, px32, py32, sx, sy, own, relx, rely, finx, finy,
    ready, w_sem, x_sem, swap_send, swap_recv, send, ag_recv, fw_recv, d_recv, plain_recv, f_recv,
):
    half = wg_hbm.shape[1]
    width = wd_hbm.shape[1]
    tiles = half // TILE

    me = lax.axis_index("tp")
    core = me % 2
    iy = (me // 2) % 2
    ix = me // 4
    nx = (me + 4) % 8
    ny = me + 2 - 4 * iy
    sib = me + 1 - 2 * core

    barrier = pltpu.get_barrier_semaphore()
    pairs = ((ix, nx, 0), (iy, ny, 1), (1 - core, sib, 2))

    for late, d, _ in pairs:
        @pl.when(late == 0)
        def _():
            pl.semaphore_signal(barrier, inc=1, device_id={"tp": d}, device_id_type=MESH)

    local = [
        pltpu.make_async_copy(wg_hbm, w.at[0], w_sem),
        pltpu.make_async_copy(wu_hbm, w.at[2], w_sem),
        pltpu.make_async_copy(wd_hbm, wd.at[pl.ds(0, half)], w_sem),
    ]
    for c in local:
        c.start()
    own_x = pltpu.make_async_copy(x_hbm, xb.at[OWN], x_sem)
    own_x.start()

    first = ix + iy + 1 - core

    @pl.when(first > 0)
    def _():
        pl.semaphore_wait(barrier, first)

    for late, d, i in pairs:
        @pl.when(late == 1)
        def _():
            pl.semaphore_signal(ready.at[i], inc=1, device_id={"tp": d}, device_id_type=MESH)

    def remote(src, dst, recv, d, sem=send):
        return pltpu.make_async_remote_copy(
            src_ref=src, dst_ref=dst, send_sem=sem, recv_sem=recv, device_id={"tp": d}, device_id_type=MESH
        )

    def rows(i):
        return pl.ds(i * SUB, SUB)

    group = (0, 1, 2, 2)
    ag_x = [remote(x_hbm.at[rows(i)], xb.at[BX, rows(i)], ag_recv.at[g], nx) for i, g in zip((0, 1, 2, 3), group)]
    ag_y = [remote(x_hbm.at[rows(i)], xb.at[BY, rows(i)], ag_recv.at[g], ny) for i, g in zip((2, 3, 0, 1), group)]
    swap = [
        remote(wg_hbm, w.at[1], swap_recv, sib, swap_send),
        remote(wu_hbm, w.at[3], swap_recv, sib, swap_send),
        remote(wd_hbm, wd.at[pl.ds(half, half)], swap_recv, sib, swap_send),
    ]
    copies = (ag_x, ag_y, swap)
    for now in (1, 0):
        for late, _, i in pairs:
            @pl.when(late == now)
            def _():
                if not now:
                    pl.semaphore_wait(ready.at[i], 1)
                for c in copies[i]:
                    c.start()

    def wait(ref, sem):
        pltpu.make_async_copy(ref, ref, sem).wait()

    fw_y = [remote(xb.at[BX, rows(k)], xb.at[BD, rows(2 * k)], fw_recv.at[k], ny) for k in range(2)]
    fw_x = [remote(xb.at[BY, rows(2 + k)], xb.at[BD, rows(2 * k + 1)], fw_recv.at[k], nx) for k in range(2)]
    pair = pl.ds(0, 2 * SUB)
    for k in range(2):
        wait(xb.at[BX, pair], ag_recv.at[k])
        fw_y[k].start()
        fw_x[k].start()

    def unit(b, u, ref, r0):
        x_ref = xb.at[b, pl.ds(u * UNIT, UNIT)]

        def hidden(n, _):
            s, col = n // tiles, pl.ds(pl.multiple_of((n % tiles) * TILE, TILE), TILE)
            gate = jnp.dot(x_ref[...], w[s, :, col], preferred_element_type=F32)
            up = jnp.dot(x_ref[...], w[2 + s, :, col], preferred_element_type=F32)
            hid[:, pl.ds(pl.multiple_of(n * TILE, TILE), TILE)] = (jax.nn.silu(gate) * up).astype(BF16)
            return _

        def down(n, _):
            cols = pl.ds(pl.multiple_of(n * TILE, TILE), TILE)
            v = jnp.dot(hid[...], wd[:, cols], preferred_element_type=F32)
            ref[pl.ds(r0, UNIT), cols] = v.astype(ref.dtype)
            return _

        lax.fori_loop(0, 2 * tiles, hidden, None)
        lax.fori_loop(0, width // TILE, down, None)

    weights = pl.ds(0, 3)
    wait(w.at[weights], w_sem)
    wait(w.at[weights], swap_recv)

    d_x = [remote(pd.at[rows(2 * k)], relx.at[rows(k)], d_recv.at[k], nx) for k in range(2)]
    d_y = [remote(pd.at[rows(2 * k + 1)], rely.at[rows(k)], d_recv.at[k], ny) for k in range(2)]
    low, high = pl.ds(0, UNIT), pl.ds(UNIT, UNIT)

    unit(BX, 0, px, 0)
    remote(px, finx.at[low], plain_recv, nx).start()
    unit(BY, 1, py, 0)
    remote(py, finy.at[high], plain_recv, ny).start()
    own_x.wait()
    unit(OWN, 0, own, 0)
    wait(xb.at[BX], ag_recv.at[2])
    unit(BX, 1, px32, 0)
    wait(xb.at[BD, pair], fw_recv.at[0])
    unit(BD, 0, pd, 0)
    d_x[0].start()
    d_y[0].start()
    unit(BY, 0, py32, 0)
    wait(xb.at[BD, pair], fw_recv.at[1])
    unit(BD, 1, pd, UNIT)
    d_x[1].start()
    d_y[1].start()
    unit(OWN, 1, own, UNIT)

    wait(finx, plain_recv)
    own[low] += finx[low].astype(F32)
    own[high] += finy[high].astype(F32)

    for i, (r0, n, k) in enumerate(RELAY):
        if i == 0 or k != RELAY[i - 1][2]:
            wait(relx.at[pair], d_recv.at[k])
        r = pl.ds(r0, n)
        sy[r] = (py32[r] + relx[r].astype(F32)).astype(BF16)
        remote(sy.at[r], finy.at[r], f_recv.at[i], ny).start()
        sx[r] = (px32[r] + rely[r].astype(F32)).astype(BF16)
        remote(sx.at[r], finx.at[pl.ds(UNIT + r0, n)], f_recv.at[i], nx).start()

    wait(w.at[weights], swap_send)
    for i, (r0, n, _) in enumerate(RELAY):
        wait(finx.at[pl.ds(0, 2 * n)], f_recv.at[i])
        a, b = pl.ds(r0, n), pl.ds(UNIT + r0, n)
        out[a] = (own[a] + finy[a].astype(F32)).astype(BF16)
        out[b] = (own[b] + finx[b].astype(F32)).astype(BF16)
    wait(w.at[weights], send)


def solution(mesh):
    def step(x, w_gate, w_up, w_down):
        rows, depth = x.shape
        half, width = w_down.shape
        vmem = pltpu.VMEM
        dma = pltpu.SemaphoreType.DMA
        flops = 2 * 4 * rows * depth * 2 * half * 3
        return pl.pallas_call(
            kernel,
            out_shape=pltpu.VMEM((rows, width), BF16),
            in_specs=[pl.BlockSpec(memory_space=pl.ANY)] * 4,
            out_specs=pl.BlockSpec(memory_space=pltpu.VMEM),
            scratch_shapes=[
                vmem((4, depth, half), BF16),
                vmem((2 * half, width), BF16),
                vmem((4, rows, depth), BF16),
                vmem((UNIT, 2 * half), BF16),
                vmem((rows, width), BF16),
                vmem((UNIT, width), BF16),
                vmem((UNIT, width), BF16),
                vmem((UNIT, width), F32),
                vmem((UNIT, width), F32),
                vmem((UNIT, width), BF16),
                vmem((UNIT, width), BF16),
                vmem((rows, width), F32),
                vmem((UNIT, width), BF16),
                vmem((UNIT, width), BF16),
                vmem((rows, width), BF16),
                vmem((rows, width), BF16),
                pltpu.SemaphoreType.REGULAR((3,)),
                dma,
                dma,
                dma,
                dma,
                dma,
                dma((3,)),
                dma((2,)),
                dma((2,)),
                dma,
                dma((len(RELAY),)),
            ],
            compiler_params=pltpu.CompilerParams(
                collective_id=0, has_side_effects=True, vmem_limit_bytes=60 * 2**20
            ),
            cost_estimate=pl.CostEstimate(flops=flops, bytes_accessed=32 * 2**20, transcendentals=0),
            name="mlp",
        )(x, w_gate, w_up, w_down)

    return jax.shard_map(
        step,
        mesh=mesh,
        in_specs=(P(("dp", "tp"), None), P(None, "tp"), P(None, "tp"), P("tp", None)),
        out_specs=P(("dp", "tp"), None),
        check_vma=False,
    )
```

time: 142 us -> 141 us (level)
  the two profiles are of different devices: /device:TPU:0 before, /device:TPU:7 now
where the time goes in v3:
time: 141 us; the launch traced here: 138 us
  Pallas kernels  137 us (97%)
    pallas_call x1, Pallas kernels, step(): pl.pallas_call(kernel, out_shape=pltpu.VMEM((rows, width), BF16), in_spec...  137 us

profile of v3, /device:TPU:7, one launch (start us, length us, event | category | flops | bytes accessed | tf_op | source)
XLA Modules:
  0.0 137.9 jit_solution(17080754311039204846)
XLA Ops:
  0.0 136.6 %mlp.1 = bf16[512,2048]{1,0:T(8,128)(2,1)S(1)} custom-call(bf16[512,2048]{1,0:T(8,128)(2,1)} %x_hbm.1, bf16[2048,1024]{1,0:T(8,128)(2,1)} %wg_hbm.1, bf16[2048,1024]{1,0:T(8,128)(2,1)} %wu_hbm.1, bf16[1024,2048]{1,0:T(8,128)(2,1)} %wd_hbm.1), custom_call_target="tpu_custom_call" | custom-call | flops 51539607552 | bytes 33554432 | tf_op jit(solution)/shard_map/mlp/pallas_call | solution.py:179
  136.6 1.3 copy.6

commit v4 on v3

--- a/solution.py
+++ b/solution.py
@@ -15,13 +15,13 @@
 
 OWN, BX, BY, BD = 0, 1, 2, 3
 
-RELAY = ((0, 128, 0), (128, 96, 1), (224, 32, 1))
+RELAY = ((0, 32, 0), (32, 96, 0), (128, 96, 1), (224, 32, 1))
 
 
 def kernel(
     x_hbm, wg_hbm, wu_hbm, wd_hbm, out,
     w, wd, xb, hid, pd, px, py, px32, py32, sx, sy, own, relx, rely, finx, finy,
-    ready, w_sem, x_sem, swap_send, swap_recv, send, ag_recv, fw_recv, d_recv, plain_recv, f_recv,
+    ready, turn, w_sem, x_sem, swap_send, swap_recv, send, lead_send, ag_recv, fw_recv, d_recv, plain_recv, f_recv,
 ):
     half = wg_hbm.shape[1]
     width = wd_hbm.shape[1]
@@ -151,14 +151,47 @@
     own[low] += finx[low].astype(F32)
     own[high] += finy[high].astype(F32)
 
-    for i, (r0, n, k) in enumerate(RELAY):
-        if i == 0 or k != RELAY[i - 1][2]:
-            wait(relx.at[pair], d_recv.at[k])
+    def relay(i):
+        r0, n, _ = RELAY[i]
         r = pl.ds(r0, n)
         sy[r] = (py32[r] + relx[r].astype(F32)).astype(BF16)
-        remote(sy.at[r], finy.at[r], f_recv.at[i], ny).start()
         sx[r] = (px32[r] + rely[r].astype(F32)).astype(BF16)
-        remote(sx.at[r], finx.at[pl.ds(UNIT + r0, n)], f_recv.at[i], nx).start()
+        sems = (lead_send.at[0], lead_send.at[1]) if i == 0 else (send, send)
+        return (
+            remote(sx.at[r], finx.at[pl.ds(UNIT + r0, n)], f_recv.at[i], nx, sems[0]),
+            remote(sy.at[r], finy.at[r], f_recv.at[i], ny, sems[1]),
+        )
+
+    lead = pl.ds(0, RELAY[0][1])
+    wait(relx.at[pair], d_recv.at[0])
+    head, rest = relay(0), relay(1)
+
+    def go(i):
+        @pl.when(core == 1)
+        def _():
+            pl.semaphore_wait(turn.at[i], 1)
+
+        head[i].start()
+        rest[i].start()
+
+    def done(i):
+        @pl.when(core == 0)
+        def _():
+            wait(finx.at[lead], lead_send.at[i])
+            pl.semaphore_signal(turn.at[i], inc=1, device_id={"tp": sib}, device_id_type=MESH)
+
+    for early, order in ((1, (0, 1)), (0, (1, 0))):
+        @pl.when(ix == early)
+        def _():
+            for i in order:
+                go(i)
+            for i in order:
+                done(i)
+
+    wait(relx.at[pair], d_recv.at[1])
+    for i in (2, 3):
+        for c in relay(i):
+            c.start()
 
     wait(w.at[weights], swap_send)
     for i, (r0, n, _) in enumerate(RELAY):
@@ -166,7 +199,13 @@
         a, b = pl.ds(r0, n), pl.ds(UNIT + r0, n)
         out[a] = (own[a] + finy[a].astype(F32)).astype(BF16)
         out[b] = (own[b] + finx[b].astype(F32)).astype(BF16)
-    wait(w.at[weights], send)
+
+    @pl.when(core == 1)
+    def _():
+        for i in (0, 1):
+            wait(finx.at[lead], lead_send.at[i])
+
+    wait(w.at[:, pl.ds(0, 3 * half // 2 - RELAY[0][1])], send)
 
 
 def solution(mesh):
@@ -199,11 +238,13 @@
                 vmem((rows, width), BF16),
                 vmem((rows, width), BF16),
                 pltpu.SemaphoreType.REGULAR((3,)),
-                dma,
-                dma,
-                dma,
-                dma,
-                dma,
+                pltpu.SemaphoreType.REGULAR((2,)),
+                dma,
+                dma,
+                dma,
+                dma,
+                dma,
+                dma((2,)),
                 dma((3,)),
                 dma((2,)),
                 dma((2,)),

time: 141 us -> 140 us (level); the launches traced: 138 us -> 139 us
  no operation moved by 1% of the time
where the time goes in v4:
time: 140 us; the launch traced here: 139 us
  Pallas kernels  138 us (99%)
    pallas_call x1, Pallas kernels, step(): pl.pallas_call(kernel, out_shape=pltpu.VMEM((rows, width), BF16), in_spec...  138 us

profile of v4, /device:TPU:7, one launch (start us, length us, event | category | flops | bytes accessed | tf_op | source)
XLA Modules:
  0.0 139.1 jit_solution(16699751407313732818)
XLA Ops:
  0.0 137.8 %mlp.1 = bf16[512,2048]{1,0:T(8,128)(2,1)S(1)} custom-call(bf16[512,2048]{1,0:T(8,128)(2,1)} %x_hbm.1, bf16[2048,1024]{1,0:T(8,128)(2,1)} %wg_hbm.1, bf16[2048,1024]{1,0:T(8,128)(2,1)} %wu_hbm.1, bf16[1024,2048]{1,0:T(8,128)(2,1)} %wd_hbm.1), custom_call_target="tpu_custom_call" | custom-call | flops 51539607552 | bytes 33554432 | tf_op jit(solution)/shard_map/mlp/pallas_call | solution.py:218
  137.8 1.3 copy.6

commit v5 on v3

--- a/solution.py
+++ b/solution.py
@@ -15,13 +15,13 @@
 
 OWN, BX, BY, BD = 0, 1, 2, 3
 
-RELAY = ((0, 128, 0), (128, 96, 1), (224, 32, 1))
+RELAY = ((0, 32, 0), (32, 96, 0), (128, 112, 1), (240, 16, 1))
 
 
 def kernel(
     x_hbm, wg_hbm, wu_hbm, wd_hbm, out,
     w, wd, xb, hid, pd, px, py, px32, py32, sx, sy, own, relx, rely, finx, finy,
-    ready, w_sem, x_sem, swap_send, swap_recv, send, ag_recv, fw_recv, d_recv, plain_recv, f_recv,
+    ready, turn, w_sem, swap_send, swap_recv, send, lead_send, ag_recv, fw_recv, d_recv, plain_recv, f_recv,
 ):
     half = wg_hbm.shape[1]
     width = wd_hbm.shape[1]
@@ -43,26 +43,16 @@
         def _():
             pl.semaphore_signal(barrier, inc=1, device_id={"tp": d}, device_id_type=MESH)
 
-    local = [
-        pltpu.make_async_copy(wg_hbm, w.at[0], w_sem),
-        pltpu.make_async_copy(wu_hbm, w.at[2], w_sem),
-        pltpu.make_async_copy(wd_hbm, wd.at[pl.ds(0, half)], w_sem),
-    ]
-    for c in local:
-        c.start()
-    own_x = pltpu.make_async_copy(x_hbm, xb.at[OWN], x_sem)
-    own_x.start()
-
     first = ix + iy + 1 - core
 
     @pl.when(first > 0)
     def _():
         pl.semaphore_wait(barrier, first)
 
-    for late, d, i in pairs:
+    for late, d, _ in pairs:
         @pl.when(late == 1)
         def _():
-            pl.semaphore_signal(ready.at[i], inc=1, device_id={"tp": d}, device_id_type=MESH)
+            pl.semaphore_signal(ready, inc=1, device_id={"tp": d}, device_id_type=MESH)
 
     def remote(src, dst, recv, d, sem=send):
         return pltpu.make_async_remote_copy(
@@ -81,14 +71,29 @@
         remote(wd_hbm, wd.at[pl.ds(half, half)], swap_recv, sib, swap_send),
     ]
     copies = (ag_x, ag_y, swap)
-    for now in (1, 0):
+
+    def start(now):
         for late, _, i in pairs:
             @pl.when(late == now)
             def _():
-                if not now:
-                    pl.semaphore_wait(ready.at[i], 1)
                 for c in copies[i]:
                     c.start()
+
+    start(1)
+    local = [
+        pltpu.make_async_copy(wg_hbm, w.at[0], w_sem),
+        pltpu.make_async_copy(wu_hbm, w.at[2], w_sem),
+        pltpu.make_async_copy(wd_hbm, wd.at[pl.ds(0, half)], w_sem),
+        pltpu.make_async_copy(x_hbm, xb.at[OWN], w_sem),
+    ]
+    for c in local:
+        c.start()
+
+    @pl.when(first < 3)
+    def _():
+        pl.semaphore_wait(ready, 3 - first)
+
+    start(0)
 
     def wait(ref, sem):
         pltpu.make_async_copy(ref, ref, sem).wait()
@@ -121,7 +126,7 @@
         lax.fori_loop(0, width // TILE, down, None)
 
     weights = pl.ds(0, 3)
-    wait(w.at[weights], w_sem)
+    wait(w.at[:, pl.ds(0, 7 * half // 4)], w_sem)
     wait(w.at[weights], swap_recv)
 
     d_x = [remote(pd.at[rows(2 * k)], relx.at[rows(k)], d_recv.at[k], nx) for k in range(2)]
@@ -132,7 +137,6 @@
     remote(px, finx.at[low], plain_recv, nx).start()
     unit(BY, 1, py, 0)
     remote(py, finy.at[high], plain_recv, ny).start()
-    own_x.wait()
     unit(OWN, 0, own, 0)
     wait(xb.at[BX], ag_recv.at[2])
     unit(BX, 1, px32, 0)
@@ -151,14 +155,37 @@
     own[low] += finx[low].astype(F32)
     own[high] += finy[high].astype(F32)
 
-    for i, (r0, n, k) in enumerate(RELAY):
-        if i == 0 or k != RELAY[i - 1][2]:
-            wait(relx.at[pair], d_recv.at[k])
+    def relay(i):
+        r0, n, _ = RELAY[i]
         r = pl.ds(r0, n)
         sy[r] = (py32[r] + relx[r].astype(F32)).astype(BF16)
-        remote(sy.at[r], finy.at[r], f_recv.at[i], ny).start()
         sx[r] = (px32[r] + rely[r].astype(F32)).astype(BF16)
-        remote(sx.at[r], finx.at[pl.ds(UNIT + r0, n)], f_recv.at[i], nx).start()
+        sem = lead_send if i == 0 else send
+        return (
+            remote(sx.at[r], finx.at[pl.ds(UNIT + r0, n)], f_recv.at[i], nx, sem),
+            remote(sy.at[r], finy.at[r], f_recv.at[i], ny, sem),
+        )
+
+    lead = pl.ds(0, 2 * RELAY[0][1])
+    wait(relx.at[pair], d_recv.at[0])
+    head, rest = relay(0), relay(1)
+
+    @pl.when(core == 1)
+    def _():
+        pl.semaphore_wait(turn, 1)
+
+    for c in (*head, *rest):
+        c.start()
+    wait(finx.at[lead], lead_send)
+
+    @pl.when(core == 0)
+    def _():
+        pl.semaphore_signal(turn, inc=1, device_id={"tp": sib}, device_id_type=MESH)
+
+    wait(relx.at[pair], d_recv.at[1])
+    for i in (2, 3):
+        for c in relay(i):
+            c.start()
 
     wait(w.at[weights], swap_send)
     for i, (r0, n, _) in enumerate(RELAY):
@@ -166,7 +193,8 @@
         a, b = pl.ds(r0, n), pl.ds(UNIT + r0, n)
         out[a] = (own[a] + finy[a].astype(F32)).astype(BF16)
         out[b] = (own[b] + finx[b].astype(F32)).astype(BF16)
-    wait(w.at[weights], send)
+
+    wait(w.at[:, pl.ds(0, 3 * half // 2 - RELAY[0][1])], send)
 
 
 def solution(mesh):
@@ -198,7 +226,8 @@
                 vmem((UNIT, width), BF16),
                 vmem((rows, width), BF16),
                 vmem((rows, width), BF16),
-                pltpu.SemaphoreType.REGULAR((3,)),
+                pltpu.SemaphoreType.REGULAR,
+                pltpu.SemaphoreType.REGULAR,
                 dma,
                 dma,
                 dma,

time: 141 us -> 139 us (0.986); the launches traced: 138 us -> 139 us
  no operation moved by 1% of the time
where the time goes in v5:
time: 139 us
  Pallas kernels  138 us (99%)
    pallas_call x1, Pallas kernels, step(): pl.pallas_call(kernel, out_shape=pltpu.VMEM((rows, width), BF16), in_spec...  138 us

profile of v5, /device:TPU:7, one launch (start us, length us, event | category | flops | bytes accessed | tf_op | source)
XLA Modules:
  0.0 139.0 jit_solution(6640532745498921320)
XLA Ops:
  0.0 137.7 %mlp.1 = bf16[512,2048]{1,0:T(8,128)(2,1)S(1)} custom-call(bf16[512,2048]{1,0:T(8,128)(2,1)} %x_hbm.1, bf16[2048,1024]{1,0:T(8,128)(2,1)} %wg_hbm.1, bf16[2048,1024]{1,0:T(8,128)(2,1)} %wu_hbm.1, bf16[1024,2048]{1,0:T(8,128)(2,1)} %wd_hbm.1), custom_call_target="tpu_custom_call" | custom-call | flops 51539607552 | bytes 33554432 | tf_op jit(solution)/shard_map/mlp/pallas_call | solution.py:207
  137.7 1.3 copy.6

commit v6 on v5

--- a/solution.py
+++ b/solution.py
@@ -16,13 +16,21 @@
 OWN, BX, BY, BD = 0, 1, 2, 3
 
 RELAY = ((0, 32, 0), (32, 96, 0), (128, 112, 1), (240, 16, 1))
+TAIL = RELAY[-1][1]
 
 
 def kernel(
-    x_hbm, wg_hbm, wu_hbm, wd_hbm, out,
+    x_hbm, wg_hbm, wu_hbm, wd_hbm, out, tail_own, tail_fin,
     w, wd, xb, hid, pd, px, py, px32, py32, sx, sy, own, relx, rely, finx, finy,
-    ready, turn, w_sem, swap_send, swap_recv, send, lead_send, ag_recv, fw_recv, d_recv, plain_recv, f_recv,
+    ready, turn, sems,
 ):
+    ag_recv = (sems.at[0], sems.at[1], sems.at[2])
+    fw_recv = (sems.at[2], sems.at[3])
+    d_recv = (sems.at[4], sems.at[5])
+    f_recv = (sems.at[6], sems.at[6], sems.at[6], sems.at[7])
+    send, lead_send = sems.at[8], sems.at[9]
+    w_sem, swap_recv, swap_send, plain_recv = ag_recv[0], ag_recv[1], lead_send, d_recv[0]
+
     half = wg_hbm.shape[1]
     width = wd_hbm.shape[1]
     tiles = half // TILE
@@ -63,8 +71,8 @@
         return pl.ds(i * SUB, SUB)
 
     group = (0, 1, 2, 2)
-    ag_x = [remote(x_hbm.at[rows(i)], xb.at[BX, rows(i)], ag_recv.at[g], nx) for i, g in zip((0, 1, 2, 3), group)]
-    ag_y = [remote(x_hbm.at[rows(i)], xb.at[BY, rows(i)], ag_recv.at[g], ny) for i, g in zip((2, 3, 0, 1), group)]
+    ag_x = [remote(x_hbm.at[rows(i)], xb.at[BX, rows(i)], ag_recv[g], nx) for i, g in zip((0, 1, 2, 3), group)]
+    ag_y = [remote(x_hbm.at[rows(i)], xb.at[BY, rows(i)], ag_recv[g], ny) for i, g in zip((2, 3, 0, 1), group)]
     swap = [
         remote(wg_hbm, w.at[1], swap_recv, sib, swap_send),
         remote(wu_hbm, w.at[3], swap_recv, sib, swap_send),
@@ -95,14 +103,14 @@
 
     start(0)
 
-    def wait(ref, sem):
+    def wait(mib, sem):
+        ref = w.at[:, pl.ds(0, int(mib * 2**20) // (4 * 2 * half))]
         pltpu.make_async_copy(ref, ref, sem).wait()
 
-    fw_y = [remote(xb.at[BX, rows(k)], xb.at[BD, rows(2 * k)], fw_recv.at[k], ny) for k in range(2)]
-    fw_x = [remote(xb.at[BY, rows(2 + k)], xb.at[BD, rows(2 * k + 1)], fw_recv.at[k], nx) for k in range(2)]
-    pair = pl.ds(0, 2 * SUB)
+    fw_y = [remote(xb.at[BX, rows(k)], xb.at[BD, rows(2 * k)], fw_recv[k], ny) for k in range(2)]
+    fw_x = [remote(xb.at[BY, rows(2 + k)], xb.at[BD, rows(2 * k + 1)], fw_recv[k], nx) for k in range(2)]
     for k in range(2):
-        wait(xb.at[BX, pair], ag_recv.at[k])
+        wait((15, 13)[k], ag_recv[k])
         fw_y[k].start()
         fw_x[k].start()
 
@@ -125,12 +133,8 @@
         lax.fori_loop(0, 2 * tiles, hidden, None)
         lax.fori_loop(0, width // TILE, down, None)
 
-    weights = pl.ds(0, 3)
-    wait(w.at[:, pl.ds(0, 7 * half // 4)], w_sem)
-    wait(w.at[weights], swap_recv)
-
-    d_x = [remote(pd.at[rows(2 * k)], relx.at[rows(k)], d_recv.at[k], nx) for k in range(2)]
-    d_y = [remote(pd.at[rows(2 * k + 1)], rely.at[rows(k)], d_recv.at[k], ny) for k in range(2)]
+    d_x = [remote(pd.at[rows(2 * k)], relx.at[rows(k)], d_recv[k], nx) for k in range(2)]
+    d_y = [remote(pd.at[rows(2 * k + 1)], rely.at[rows(k)], d_recv[k], ny) for k in range(2)]
     low, high = pl.ds(0, UNIT), pl.ds(UNIT, UNIT)
 
     unit(BX, 0, px, 0)
@@ -138,20 +142,19 @@
     unit(BY, 1, py, 0)
     remote(py, finy.at[high], plain_recv, ny).start()
     unit(OWN, 0, own, 0)
-    wait(xb.at[BX], ag_recv.at[2])
+    wait(3, ag_recv[2])
     unit(BX, 1, px32, 0)
-    wait(xb.at[BD, pair], fw_recv.at[0])
     unit(BD, 0, pd, 0)
     d_x[0].start()
     d_y[0].start()
     unit(BY, 0, py32, 0)
-    wait(xb.at[BD, pair], fw_recv.at[1])
+    wait(1, fw_recv[1])
     unit(BD, 1, pd, UNIT)
     d_x[1].start()
     d_y[1].start()
     unit(OWN, 1, own, UNIT)
 
-    wait(finx, plain_recv)
+    wait(3, d_recv[0])
     own[low] += finx[low].astype(F32)
     own[high] += finy[high].astype(F32)
 
@@ -161,13 +164,9 @@
         sy[r] = (py32[r] + relx[r].astype(F32)).astype(BF16)
         sx[r] = (px32[r] + rely[r].astype(F32)).astype(BF16)
         sem = lead_send if i == 0 else send
-        return (
-            remote(sx.at[r], finx.at[pl.ds(UNIT + r0, n)], f_recv.at[i], nx, sem),
-            remote(sy.at[r], finy.at[r], f_recv.at[i], ny, sem),
-        )
-
-    lead = pl.ds(0, 2 * RELAY[0][1])
-    wait(relx.at[pair], d_recv.at[0])
+        to_x, to_y = (finx.at[pl.ds(UNIT + r0, n)], finy.at[r]) if i < 3 else (tail_fin.at[1], tail_fin.at[0])
+        return remote(sx.at[r], to_x, f_recv[i], nx, sem), remote(sy.at[r], to_y, f_recv[i], ny, sem)
+
     head, rest = relay(0), relay(1)
 
     @pl.when(core == 1)
@@ -176,25 +175,35 @@
 
     for c in (*head, *rest):
         c.start()
-    wait(finx.at[lead], lead_send)
+    wait(12.25, lead_send)
 
     @pl.when(core == 0)
     def _():
         pl.semaphore_signal(turn, inc=1, device_id={"tp": sib}, device_id_type=MESH)
 
-    wait(relx.at[pair], d_recv.at[1])
+    wait(1, d_recv[1])
     for i in (2, 3):
         for c in relay(i):
             c.start()
 
-    wait(w.at[weights], swap_send)
-    for i, (r0, n, _) in enumerate(RELAY):
-        wait(finx.at[pl.ds(0, 2 * n)], f_recv.at[i])
-        a, b = pl.ds(r0, n), pl.ds(UNIT + r0, n)
-        out[a] = (own[a] + finy[a].astype(F32)).astype(BF16)
-        out[b] = (own[b] + finx[b].astype(F32)).astype(BF16)
-
-    wait(w.at[:, pl.ds(0, 3 * half // 2 - RELAY[0][1])], send)
+    wait(2 - TAIL / SUB, f_recv[0])
+    for u, ref in ((0, finy), (1, finx)):
+        r = pl.ds(u * UNIT, UNIT - TAIL)
+        out[r] = (own[r] + ref[r].astype(F32)).astype(BF16)
+        tail_own[u] = own[pl.ds((u + 1) * UNIT - TAIL, TAIL)]
+    wait(TAIL / SUB, f_recv[3])
+    wait(11.75, send)
+
+
+def put(y, tail_own, tail_fin, out, tail, sem):
+    step = 8
+    for r in range(0, out.shape[0], step):
+        if r % UNIT < UNIT - TAIL:
+            pltpu.make_async_copy(y.at[pl.ds(r, step)], out.at[pl.ds(r, step)], sem).start()
+    tail[...] = (tail_own[...] + tail_fin[...].astype(F32)).astype(BF16)
+    for u in range(2):
+        pltpu.make_async_copy(tail.at[u], out.at[pl.ds((u + 1) * UNIT - TAIL, TAIL)], sem).start()
+    pltpu.make_async_copy(y, y, sem).wait()
 
 
 def solution(mesh):
@@ -204,11 +213,11 @@
         vmem = pltpu.VMEM
         dma = pltpu.SemaphoreType.DMA
         flops = 2 * 4 * rows * depth * 2 * half * 3
-        return pl.pallas_call(
+        parts = pl.pallas_call(
             kernel,
-            out_shape=pltpu.VMEM((rows, width), BF16),
+            out_shape=(vmem((rows, width), BF16), vmem((2, TAIL, width), F32), vmem((2, TAIL, width), BF16)),
             in_specs=[pl.BlockSpec(memory_space=pl.ANY)] * 4,
-            out_specs=pl.BlockSpec(memory_space=pltpu.VMEM),
+            out_specs=(pl.BlockSpec(memory_space=vmem),) * 3,
             scratch_shapes=[
                 vmem((4, depth, half), BF16),
                 vmem((2 * half, width), BF16),
@@ -228,23 +237,23 @@
                 vmem((rows, width), BF16),
                 pltpu.SemaphoreType.REGULAR,
                 pltpu.SemaphoreType.REGULAR,
-                dma,
-                dma,
-                dma,
-                dma,
-                dma,
-                dma((3,)),
-                dma((2,)),
-                dma((2,)),
-                dma,
-                dma((len(RELAY),)),
+                dma((10,)),
             ],
             compiler_params=pltpu.CompilerParams(
-                collective_id=0, has_side_effects=True, vmem_limit_bytes=60 * 2**20
+                collective_id=0, has_side_effects=True, vmem_limit_bytes=57 * 2**20
             ),
             cost_estimate=pl.CostEstimate(flops=flops, bytes_accessed=32 * 2**20, transcendentals=0),
             name="mlp",
         )(x, w_gate, w_up, w_down)
+        return pl.pallas_call(
+            put,
+            out_shape=jax.ShapeDtypeStruct((rows, width), BF16),
+            in_specs=[pl.BlockSpec(memory_space=vmem)] * 3,
+            out_specs=pl.BlockSpec(memory_space=pl.ANY),
+            scratch_shapes=[vmem((2, TAIL, width), BF16), dma],
+            compiler_params=pltpu.CompilerParams(vmem_limit_bytes=4 * 2**20),
+            name="put",
+        )(*(pltpu.with_memory_space_constraint(a, vmem) for a in parts))
 
     return jax.shard_map(
         step,

time: 139 us -> 139 us (level)
    pallas_call x1 -> x2, Pallas kernels: 138 us -> 139 us  [the longest x1 138 us: step(): pl.pallas_call(kernel, out_shape=(vmem((rows, width), BF16), vmem((2, TAI...]
where the time goes in v6:
time: 139 us
  Pallas kernels  139 us (100%)
    pallas_call x1, Pallas kernels, step(): pl.pallas_call(kernel, out_shape=(vmem((rows, width), BF16), vmem((2, TAI...  138 us

profile of v6, /device:TPU:7, one launch (start us, length us, event | category | flops | bytes accessed | tf_op | source)
XLA Modules:
  0.0 138.9 jit_solution(2039616128006564160)
XLA Ops:
  0.0 137.6 %mlp.1 = (bf16[512,2048]{1,0:T(8,128)(2,1)S(1)}, f32[2,16,2048]{2,1,0:T(8,128)S(1)}, bf16[2,16,2048]{2,1,0:T(8,128)(2,1)S(1)}) custom-call(bf16[512,2048]{1,0:T(8,128)(2,1)} %x_hbm.1, bf16[2048,1024]{1,0:T(8,128)(2,1)} %wg_hbm.1, bf16[2048,1024]{1,0:T(8,128)(2,1)} %wu_hbm.1, bf16[1024,2048]{1,0:T(8,128)(2,1)} %wd_hbm.1), custom_call_target="tpu_custom_call" | custom-call | flops 51539607552 | bytes 33554432 | tf_op jit(solution)/shard_map/mlp/pallas_call | solution.py:216
  137.6 1.3 put.1
